TPU v7x, 256 devices: a whole 4x4x8 slice. The times are simulated.
256 devices in a mesh: gx: 32 (over z, y_hi, core), gy: 8 (over y_lo, x).
Axes of the slice: x: 4, y: 4 (y_hi: 2, y_lo: 2; y = y_hi * 2 + y_lo), z: 8, core: 2. Of those that a mesh axis runs over, the one named last changes fastest.
Arguments:
- prognostic_values: float32 [3, 6, 4096, 4096], P(None, None, 'gx', 'gy'), may hold values from -6 to 6
- forcing_host_values: bfloat16 [3, 6, 4096, 4096], P(None, None, 'gx', 'gy'), may hold values from -6 to 6
- strength: float32 [3, 6], replicated, may hold values from 50 to 200
- level_height: float32 [3], replicated, may hold values from 0.2 to 3
- pbl_height: float32 [4096, 4096], P('gx', 'gy'), may hold values from 0.2 to 3
Outputs:
- tendency: bfloat16 [3, 6, 4096, 4096], P(None, None, 'gx', 'gy')
- energy: float32 [3, 6], replicated
All inputs are finite; a program needn't handle non-finite values.
Results may differ from a plain program's by a relative error of at most 0.001.
Values sent between devices are 32-bit elements; how exact they have to be, the bound alone decides.
A program may use at most 64 MiB of HBM per device.

v0:
```python
import jax
import jax.numpy as jnp
from jax import lax
from jax.sharding import PartitionSpec as P

KX = 32
KY = 32


ramp_depth = 0.25


def from_everyone(value, axis):
    copies = jnp.broadcast_to(value, (lax.axis_size(axis), *value.shape))
    return lax.all_to_all(copies, axis, split_axis=0, concat_axis=0, tiled=True)


def taken_together(value, axis):
    everything = from_everyone(value, axis)
    return jnp.sum(everything, axis=0)


def padded_to(lines, devices):
    spare = -lines.shape[0] % devices
    if not spare:
        return lines
    return jnp.concatenate([lines, jnp.zeros((spare, *lines.shape[1:]), lines.dtype)])


def laid_out(blocks, dim):
    lengths = list(blocks.shape[1:])
    lengths[dim] *= blocks.shape[0]
    return jnp.moveaxis(blocks, 0, dim).reshape(lengths)


def gather_directly(value, axis, dim):
    return laid_out(from_everyone(value, axis), dim)


def in_blocks(value, dim, devices):
    lengths = value.shape
    blocks = value.reshape(*lengths[:dim], devices, lengths[dim] // devices, *lengths[dim + 1 :])
    return jnp.moveaxis(blocks, dim, 0)


def summed_on_arrival(value, axis, dim):
    devices = lax.axis_size(axis)
    blocks = lax.all_to_all(in_blocks(value, dim, devices), axis, 0, 0, tiled=True)
    return jnp.sum(blocks, axis=0)


def sum_by_parts(value, axes):
    lines = value.reshape(-1, value.shape[-1])
    padded = padded_to(lines, lax.axis_size(axes))
    whole = gather_directly(summed_on_arrival(padded, axes, 0), axes, 0)
    return lax.slice_in_dim(whole, 0, len(lines)).reshape(value.shape)


def cosine_table(total, modes, start, count):
    index = (start + jnp.arange(count)).astype(jnp.float32)
    waves = jnp.arange(modes).astype(jnp.float32)
    scales = jnp.where(waves == 0.0, jnp.sqrt(1.0 / total), jnp.sqrt(2.0 / total)).astype(
        jnp.float32
    )
    return scales[None, :] * jnp.cos(jnp.pi * (index[:, None] + 0.5) * waves[None, :] / total)


def per_device(prognostic_values, forcing_host_values, strength, level_height, pbl_height):
    rows = prognostic_values.shape[2]
    cols = prognostic_values.shape[3]
    largest_wavenumber = lax.Precision.HIGHEST
    row_table = cosine_table(rows * lax.axis_size("gx"), KX, lax.axis_index("gx") * rows, rows)
    col_table = cosine_table(cols * lax.axis_size("gy"), KY, lax.axis_index("gy") * cols, cols)
    diff = forcing_host_values.astype(jnp.float32) - prognostic_values
    part = jnp.einsum("...ij,jb->...ib", diff, col_table, precision=largest_wavenumber)
    within = taken_together(
        jnp.einsum("ia,...ib->...ab", row_table, part, precision=largest_wavenumber), "gy"
    )
    mode_factors = sum_by_parts(within, "gx")
    restored_fields = jnp.einsum(
        "ia,lvab->lvib", row_table, mode_factors, precision=largest_wavenumber
    )
    recon = jnp.einsum("lvib,jb->lvij", restored_fields, col_table, precision=largest_wavenumber)
    damping_share = 1.0 / (
        1.0 + jnp.exp(-(level_height[:, None, None] - pbl_height[None]) / ramp_depth)
    )
    tendency = (strength[:, :, None, None] * damping_share[:, None] * recon).astype(jnp.bfloat16)
    energy = jnp.sum(mode_factors * mode_factors, axis=(2, 3)) / (KX * KY)
    return (tendency, energy)


def solution(mesh):
    return jax.shard_map(
        per_device,
        mesh=mesh,
        in_specs=(P(None, None, "gx", "gy"), P(None, None, "gx", "gy"), P(), P(), P("gx", "gy")),
        out_specs=(P(None, None, "gx", "gy"), P()),
        check_vma=False,
    )
```

profile of v0, /device:TPU:1, one launch (start us, length us, event | category | flops | bytes accessed | tf_op | source)
XLA Modules:
  0.0 76.3 jit_solution(3102247311464418814)
XLA Ops:
  0.7 7.3 %fusion = f32[3,6,128,32]{2,3,1,0:T(8,128)S(1)} fusion(f32[3,6,128,512]{3,2,1,0:T(8,128)} %param.5, bf16[3,6,128,512]{3,2,1,0:T(8,128)(2,1)} %param.6, f32[32]{0:T(128)S(1)} %iota_convert_fusion, f32[512]{0:T(512)S(1)} %add_multiply_fusion, f32[32]{0:T(128)S(1)} %compare_select_fusion), kind=kOutput, calls=%fused_computation.1 | convolution fusion | flops 455393280 | bytes 7375104 | tf_op jit(solution)/shard_map/...ij,jb->...ib/dot_general | solution.py:75
  8.0 0.5 convolution_bitcast_fusion.1
  8.5 0.1 copy.9
  8.6 0.3 broadcast_in_dim.28
  8.9 1.0 %reshape.42 = f32[8,1,18432]{2,1,0:T(1,128)S(1)} reshape(f32[8,3,6,32,32]{4,3,2,1,0:T(8,128)S(1)} %broadcast_in_dim.28) | data formatting | bytes 1179648
  10.0 15.3 %all_to_all.15 = f32[8,1,18432]{2,1,0:T(1,128)S(1)} all-to-all(f32[8,1,18432]{2,1,0:T(1,128)S(1)} %reshape.42), channel_id=1, replica_groups=mesh['gx'=32,'gy'=8] {'gy'}, dimensions={0} | all-to-all | bytes 1179648 | tf_op jit(solution)/shard_map/all_to_all | solution.py:15
  25.3 0.5 broadcast.82
  25.8 2.0 %reduce.2 = f32[8,18432]{1,0:T(8,128)S(1)} reduce(f32[8,1,18432]{2,1,0:T(1,128)S(1)} %all_to_all.15, f32[]{:T(128)} %broadcast.82), dimensions={1}, to_apply=%all_to_all.9.reduce_sub_computation | reduce | bytes 1179652 | tf_op jit(solution)/shard_map/all_to_all | solution.py:15
  27.9 0.0 copy-start
  27.9 0.0 copy-start.1
  27.9 0.8 %reshape.43 = f32[8,3,6,32,32]{4,3,2,1,0:T(8,128)S(1)} reshape(f32[8,18432]{1,0:T(8,128)S(1)} %reduce.2) | data formatting | bytes 1179648
  28.7 0.0 copy-start.2
  28.7 0.3 reduce_sum.34
  29.0 0.2 reshape.44
  29.2 22.9 %all_to_all.16 = f32[32,1,576]{2,1,0:T(1,128)S(1)} all-to-all(f32[32,1,576]{2,1,0:T(1,128)S(1)} %reshape.44), channel_id=1, replica_groups=mesh['gx'=32,'gy'=8] {'gx'}, dimensions={0} | all-to-all | bytes 147456 | tf_op jit(solution)/shard_map/all_to_all | solution.py:48
  52.1 0.8 %reduce.3 = f32[32,576]{1,0:T(8,128)S(1)} reduce(f32[32,1,576]{2,1,0:T(1,128)S(1)} %all_to_all.16, f32[]{:T(128)} %broadcast.82), dimensions={1}, to_apply=%all_to_all.10.reduce_sub_computation | reduce | bytes 147460 | tf_op jit(solution)/shard_map/all_to_all | solution.py:48
  53.0 0.1 reshape.45
  53.2 0.8 %reshape.46 = f32[32,1,576]{2,1,0:T(1,128)} reshape(f32[32,18,32]{2,1,0:T(8,128)S(1)} %broadcast_in_dim.29) | data formatting | bytes 147456
  54.0 3.8 %all-to-all-start.2 = ((f32[32,1,576]{2,1,0:T(1,128)}), f32[32,1,576]{2,1,0:T(1,128)S(1)}, u32[]{:S(2)}, u32[]{:S(2)}) async-start(f32[32,1,576]{2,1,0:T(1,128)} %reshape.46), calls=%async_computation.2 | async-start | bytes 163840 | tf_op jit(solution)/shard_map/all_to_all | solution.py:15
  57.9 0.0 copy-done
  57.9 0.0 copy-done.1
  57.9 0.3 add_divide_fusion
  58.2 9.8 %all-to-all-done.2 = f32[32,1,576]{2,1,0:T(1,128)S(1)} async-done(((f32[32,1,576]{2,1,0:T(1,128)}), f32[32,1,576]{2,1,0:T(1,128)S(1)}, u32[]{:S(2)}, u32[]{:S(2)}) %all-to-all-start.2) | async-done | bytes 73760 | tf_op jit(solution)/shard_map/all_to_all | solution.py:15
  67.9 0.8 %reduce.4 = f32[32,576]{1,0:T(8,128)S(1)} reduce(f32[32,1,576]{2,1,0:T(1,128)S(1)} %all-to-all-done.2, f32[]{:T(128)} %broadcast.82), dimensions={1}, to_apply=%all_to_all.11.reduce_sub_computation | reduce | bytes 147460 | tf_op jit(solution)/shard_map/all_to_all | solution.py:15
  68.8 0.1 reshape.47
  68.9 0.2 multiply_reduce_fusion
  69.1 0.1 reduce_sum.37
  69.2 0.1 reduce_sum.38
  69.3 0.7 convolution_bitcast_fusion
  70.0 0.6 broadcast_multiply_fusion
  70.6 0.0 copy-done.2
  70.6 5.7 %multiply_convert_fusion = bf16[3,6,128,512]{3,2,1,0:T(8,128)(2,1)} fusion(f32[3,128,512]{2,1,0:T(8,128)S(1)} %add_divide_fusion, f32[3,6]{1,0:T(4,128)S(1)} %copy-done.2, f32[3,6,128,32]{2,3,1,0:T(8,128)S(1)} %convolution_bitcast_fusion, f32[32]{0:T(128)S(1)} %iota_convert_fusion, f32[512]{0:T(512)S(1)} %add_multiply_fusion, f32[32]{0:T(128)S(1)} %compare_select_fusion), kind=kOutput, calls=%fused_computation | convolution fusion | flops 456572928 | bytes 3443016 | tf_op jit(solution)/shard_map/lvib,jb->lvij/dot_general | solution.py:83
  (8 shorter events, 0.2 us)
Async XLA Ops:
  27.9 30.0 %copy-start = (f32[128,512]{1,0:T(8,128)S(1)}, f32[128,512]{1,0:T(8,128)}, u32[]{:S(2)}) copy-start(f32[128,512]{1,0:T(8,128)} %param.9) | copy-start | bytes 786436
  27.9 30.0 %copy-start.1 = (f32[3]{0:T(128)S(1)}, f32[3]{0:T(128)}, u32[]{:S(2)}) copy-start(f32[3]{0:T(128)} %param.8) | copy-start | bytes 40
  28.7 41.9 %copy-start.2 = (f32[3,6]{1,0:T(4,128)S(1)}, f32[3,6]{1,0:T(4,128)}, u32[]{:S(2)}) copy-start(f32[3,6]{1,0:T(4,128)} %param.7) | copy-start | bytes 220
  54.0 13.9 %all-to-all-start.2 = ((f32[32,1,576]{2,1,0:T(1,128)}), f32[32,1,576]{2,1,0:T(1,128)S(1)}, u32[]{:S(2)}, u32[]{:S(2)}) async-start(f32[32,1,576]{2,1,0:T(1,128)} %reshape.46), calls=%async_computation.2 | async-start | bytes 163840 | tf_op jit(solution)/shard_map/all_to_all | solution.py:15
where the time goes:
time: 76.6 us; the launch traced here: 76.3 us
  blocking collectives  38.3 us (50%)
  matrix products  14.2 us (19%)
  waiting for transfers between devices  9.77 us (13%)
  other arithmetic  5.2 us (7%)
  local copies, waits for them, and re-layouts  4.16 us (5%)
  starting transfers between devices  3.85 us (5%)
  between operations  0.87 us (1%)
    all_to_all x1, blocking collectives, summed_on_arrival(): lax.all_to_all(in_blocks(value, dim, devices), axis, 0, 0, tiled=True)  22.9 us
    all_to_all x1, blocking collectives, from_everyone(): return lax.all_to_all(copies, axis, split_axis=0, concat_axis=0, tiled=True)  15.3 us
    all_to_all x1, waiting for transfers between devices, from_everyone(): return lax.all_to_all(copies, axis, split_axis=0, concat_axis=0, tiled=True)  9.77 us
    dot_general x1, matrix products, per_device(): jnp.einsum('...ij,jb->...ib', diff, col_table, precision=largest_wavenumber)  7.28 us
    dot_general x1, matrix products, per_device(): jnp.einsum('lvib,jb->lvij', restored_fields, col_table, precision=largest...  5.74 us
    all_to_all x1, starting transfers between devices, from_everyone(): return lax.all_to_all(copies, axis, split_axis=0, concat_axis=0, tiled=True)  3.85 us
    unnamed x12, local copies, waits for them, and re-layouts  3.05 us
    all_to_all x2, other arithmetic, from_everyone(): return lax.all_to_all(copies, axis, split_axis=0, concat_axis=0, tiled=True)  2.88 us
  transfers between devices with their start and end apart: 1, of which 1 were waited for; matrix products, arithmetic and copies ran while one was open for 0% of the time, Pallas kernels for 0%

commit v1 on v0

v1 whole, which is shorter than its diff:
```python
import functools

import jax
import jax.numpy as jnp
from jax import lax
from jax.experimental import pallas as pl
from jax.experimental.pallas import tpu as pltpu
from jax.sharding import PartitionSpec as P

MODES = 32
FIELDS = 18
VARS = 6
LEVELS = 3
GROUPS = 5
ROWS = 128
COLS = 512
PLANES = 8
PLANE = 32
ramp_depth = 0.25
f32 = jnp.float32
bf16 = jnp.bfloat16


def fields_of(group):
    return range(4 * group, min(4 * group + 4, FIELDS))


def owner_of(group, block):
    x, y = block, (block + group) % 4
    core = 0 if group == 0 else 1
    return (y // 2) * 2 + core, (y % 2) * 4 + x


def cosines(position, mode, total):
    turn = ((2 * position + 1) * mode) & (4 * total - 1)
    turn = jnp.minimum(turn, 4 * total - turn)
    back = turn > total
    turn = jnp.where(back, 2 * total - turn, turn)
    steep = 2 * turn > total
    angle = jnp.where(steep, total - turn, turn).astype(f32) * (jnp.pi / (2 * total))
    square = angle * angle
    even = 1.0 + square * (-0.5 + square * (1 / 24 + square * (-1 / 720 + square * (1 / 40320))))
    odd = angle * (1.0 + square * (-1 / 6 + square * (1 / 120 + square * (-1 / 5040 + square * (1 / 362880)))))
    value = jnp.where(steep, odd, even)
    value = jnp.where(back, -value, value)
    scale = jnp.where(mode == 0, (1.0 / total) ** 0.5, (2.0 / total) ** 0.5).astype(f32)
    return scale * value


def split(value):
    high = value.astype(bf16)
    return high, (value - high.astype(f32)).astype(bf16)


def iota(shape, dim):
    return lax.broadcasted_iota(jnp.int32, shape, dim)


def kernel(
    prog_hbm, forc_hbm, strength, height, pbl_hbm, out, energy_ref,
    prog, forc, pbl, weight, first_table, row_left, row_right, last_table,
    part, planes_in, totals_in, coefs,
    prog_sem, forc_sem, pbl_sem, sent1, got1, sent2, got2, sent3, got3,
):
    gx, gy = lax.axis_index("gx"), lax.axis_index("gy")
    z, place = gx // 4, gx % 4
    core, x = place % 2, gy % 4
    y = (place // 2) * 2 + gy // 4
    mine = place * 8 + gy
    lag = (y - x + 4) % 4
    group_own = jnp.where(core == 0, 0, jnp.where(lag == 0, 4, lag))
    owner = (core == 1) | (lag == 0)

    def loads(f):
        l, v = divmod(f, VARS)
        return (
            pltpu.make_async_copy(prog_hbm.at[l, v], prog.at[f], prog_sem.at[f]),
            pltpu.make_async_copy(forc_hbm.at[l, v], forc.at[f], forc_sem.at[f]),
        )

    for f in range(FIELDS):
        for copy in loads(f):
            copy.start()
    load_pbl = pltpu.make_async_copy(pbl_hbm, pbl, pbl_sem)
    load_pbl.start()

    barrier = pltpu.get_barrier_semaphore()

    def greet_plane(k, _):
        peer = (mine + k) % PLANE
        pl.semaphore_signal(
            barrier, inc=1, device_id={"gx": z * 4 + peer // 8, "gy": peer % 8},
            device_id_type=pl.DeviceIdType.MESH,
        )
        return _

    def greet_planes(k, _):
        pl.semaphore_signal(
            barrier, inc=1, device_id={"gx": ((z + k) % PLANES) * 4 + place, "gy": gy},
            device_id_type=pl.DeviceIdType.MESH,
        )
        return _

    lax.fori_loop(1, PLANE, greet_plane, 0)
    lax.fori_loop(1, PLANES, greet_planes, 0)

    for piece in range(4):
        rows = pl.ds(piece * 128, 128)
        table = cosines(gy * COLS + piece * 128 + iota((128, 128), 0), iota((128, 128), 1) % MODES, 4096)
        high, low = split(table)
        first_table[rows, 0:128] = high
        first_table[rows, 128:256] = low
        table = cosines(gy * COLS + piece * 128 + iota((128, 128), 1), iota((128, 128), 0) % MODES, 4096)
        high, low = split(table)
        last_table[:, piece * 128 : piece * 128 + 128] = jnp.where(iota((128, 128), 0) < 64, high.astype(f32), low.astype(f32)).astype(bf16)
    table = cosines(gx * ROWS + iota((32, 128), 1), iota((32, 128), 0), 4096)
    high, low = split(table)
    row_left[...] = jnp.concatenate([high, high, low, low], axis=1)
    table = cosines(gx * ROWS + iota((128, 128), 0), iota((128, 128), 1) % MODES, 4096)
    high, low = split(table)
    row_right[...] = jnp.where(iota((128, 128), 1) < 64, high.astype(f32), low.astype(f32)).astype(bf16)

    lane_block = iota((ROWS, 128), 1) // MODES

    def forward(group):
        packed = jnp.zeros((ROWS, 128), f32)
        for q, f in enumerate(fields_of(group)):
            for copy in loads(f):
                copy.wait()
            diff = forc[f].astype(f32) - prog[f]
            high, low = split(diff)
            both = jnp.dot(high, first_table[...], preferred_element_type=f32) + jnp.dot(
                low, first_table[...], preferred_element_type=f32
            )
            packed = jnp.where(lane_block == q, both[:, :128] + both[:, 128:], packed)
        high, low = split(packed)
        stacked = jnp.concatenate([high, low, high, low], axis=0)
        result = jnp.dot(row_left[...], stacked, preferred_element_type=f32)
        for block in range(4):
            part[group, block] = result[block * 8 : block * 8 + 8]

    def send_parts(group):
        for block in range(4):
            to_place, to_gy = owner_of(group, block)
            @pl.when(mine != to_place * 8 + to_gy)
            def _():
                pltpu.make_async_remote_copy(
                    part.at[group, block], planes_in.at[mine], sent1, got1,
                    device_id={"gx": z * 4 + to_place, "gy": to_gy}, device_id_type=pl.DeviceIdType.MESH,
                ).start()

    for group in range(GROUPS):
        forward(group)
        if group == 0:
            pl.semaphore_wait(barrier, PLANE - 1 + PLANES - 1)
        send_parts(group)

    load_pbl.wait()
    for l in range(LEVELS):
        weight[l] = 1.0 / (1.0 + jnp.exp(-(height[l] - pbl[...]) / ramp_depth))

    def arrived(ref, count, sem):
        whole = ref.at[pl.ds(0, count)]
        pltpu.make_async_copy(whole, whole, sem).wait()

    unit_own = group_own * 4 + x

    @pl.when(owner)
    def _():
        planes_in[mine] = part[group_own, x]
        arrived(planes_in, PLANE - 1, got1)
        sums = [planes_in[k] for k in range(PLANE)]
        while len(sums) > 1:
            sums = [a + b for a, b in zip(sums[::2], sums[1::2])]
        totals_in[z] = sums[0]
        for k in range(1, PLANES):
            pltpu.make_async_remote_copy(
                totals_in.at[z], totals_in.at[z], sent2, got2,
                device_id={"gx": ((z + k) % PLANES) * 4 + place, "gy": gy}, device_id_type=pl.DeviceIdType.MESH,
            ).start()
        arrived(totals_in, PLANES - 1, got2)
        sums = [totals_in[k] for k in range(PLANES)]
        while len(sums) > 1:
            sums = [a + b for a, b in zip(sums[::2], sums[1::2])]
        coefs[unit_own] = sums[0]

        def send_total(k, _):
            peer = (mine + k) % PLANE
            pltpu.make_async_remote_copy(
                coefs.at[unit_own], coefs.at[unit_own], sent3, got3.at[group_own],
                device_id={"gx": z * 4 + peer // 8, "gy": peer % 8}, device_id_type=pl.DeviceIdType.MESH,
            ).start()
            return _

        lax.fori_loop(1, PLANE, send_total, 0)

    spot_row, spot_col = iota((LEVELS, VARS), 0), iota((LEVELS, VARS), 1)
    block_lanes = iota((MODES, 128), 1) // MODES
    energies = jnp.zeros((LEVELS, VARS), f32)
    for group in range(GROUPS):
        holds = owner & (group_own == group)

        @pl.when(holds)
        def _():
            arrived(coefs, 3, got3.at[group])

        @pl.when(jnp.logical_not(holds))
        def _():
            arrived(coefs, 4, got3.at[group])

        coef = jnp.concatenate([coefs[4 * group + block] for block in range(4)], axis=0)
        for q, f in enumerate(fields_of(group)):
            l, v = divmod(f, VARS)
            only = jnp.where(block_lanes == q, coef, 0.0)
            total = jnp.sum(only * only, axis=(0, 1), keepdims=True) * (1.0 / (MODES * MODES))
            energies = jnp.where((spot_row == l) & (spot_col == v), total, energies)
            four = only + pltpu.roll(only, 64, 1)
            four = four + pltpu.roll(four, 32, 1)
            high, low = split(four)
            stacked = jnp.concatenate([high, low, high, low], axis=0)
            along = jnp.dot(row_right[...], stacked, preferred_element_type=f32)
            high, low = split(along)
            left = jnp.where(lane_block % 2 == 0, high.astype(f32), low.astype(f32)).astype(bf16)
            recon = jnp.dot(left, last_table[...], preferred_element_type=f32)
            out[l, v] = ((strength[l, v] * weight[l]) * recon).astype(bf16)
    energy_ref[...] = energies

    @pl.when(owner)
    def _():
        flat = pltpu.make_async_copy(part.at[pl.ds(0, 4)], part.at[pl.ds(0, 4)], sent1)
        flat.wait()
        rest = part.at[4, pl.ds(0, 3)]
        pltpu.make_async_copy(rest, rest, sent1).wait()
        arrived(totals_in, PLANES - 1, sent2)
        arrived(planes_in, PLANE - 1, sent3)

    @pl.when(jnp.logical_not(owner))
    def _():
        pltpu.make_async_copy(part, part, sent1).wait()


def per_device(prognostic_values, forcing_host_values, strength, level_height, pbl_height):
    hbm = pl.BlockSpec(memory_space=pltpu.HBM)
    smem = pl.BlockSpec(memory_space=pltpu.SMEM)
    vmem = pl.BlockSpec(memory_space=pltpu.VMEM)
    dma = pltpu.SemaphoreType.DMA
    return pl.pallas_call(
        kernel,
        out_shape=(
            jax.ShapeDtypeStruct((LEVELS, VARS, ROWS, COLS), bf16),
            jax.ShapeDtypeStruct((LEVELS, VARS), f32),
        ),
        in_specs=[hbm, hbm, smem, smem, hbm],
        out_specs=(vmem, vmem),
        scratch_shapes=[
            pltpu.VMEM((FIELDS, ROWS, COLS), f32),
            pltpu.VMEM((FIELDS, ROWS, COLS), bf16),
            pltpu.VMEM((ROWS, COLS), f32),
            pltpu.VMEM((LEVELS, ROWS, COLS), f32),
            pltpu.VMEM((COLS, 256), bf16),
            pltpu.VMEM((MODES, 512), bf16),
            pltpu.VMEM((ROWS, 128), bf16),
            pltpu.VMEM((128, COLS), bf16),
            pltpu.VMEM((GROUPS, 4, 8, 128), f32),
            pltpu.VMEM((PLANE, 8, 128), f32),
            pltpu.VMEM((PLANES, 8, 128), f32),
            pltpu.VMEM((GROUPS * 4, 8, 128), f32),
            dma((FIELDS,)), dma((FIELDS,)), dma(()),
            dma(()), dma(()), dma(()), dma(()), dma(()), dma((GROUPS,)),
        ],
        compiler_params=pltpu.CompilerParams(
            collective_id=0, has_side_effects=True, vmem_limit_bytes=40 * 1024 * 1024
        ),
    )(prognostic_values, forcing_host_values, strength, level_height, pbl_height)


def solution(mesh):
    return jax.shard_map(
        per_device,
        mesh=mesh,
        in_specs=(P(None, None, "gx", "gy"), P(None, None, "gx", "gy"), P(), P(), P("gx", "gy")),
        out_specs=(P(None, None, "gx", "gy"), P()),
        check_vma=False,
    )
```

time: 76.6 us -> 43.4 us (0.57)
  blocking collectives: 38.3 us -> 0 us
  Pallas kernels: 0 us -> 34.3 us
  matrix products: 14.2 us -> 0 us
  waiting for transfers between devices: 9.77 us -> 0 us
  other arithmetic: 5.2 us -> 0 us
  local copies, waits for them, and re-layouts: 4.16 us -> 8.27 us
  starting transfers between devices: 3.85 us -> 0 us
    all_to_all x2 -> x0, blocking collectives: 38.3 us -> none  [the longest x1 22.9 us: summed_on_arrival(): lax.all_to_all(in_blocks(value, dim, devices), axis, 0, 0, tiled=True)]
    pallas_call x0 -> x1, Pallas kernels: none -> 34.3 us  [per_device(): pl.pallas_call(kernel, out_shape=(jax.ShapeDtypeStruct((LEVELS, VARS, ROW...]
    dot_general x4 -> x0, matrix products: 14.2 us -> none  [the longest x1 7.28 us: per_device(): jnp.einsum('...ij,jb->...ib', diff, col_table, precision=largest_wavenumber)]
    all_to_all x1 -> x0, waiting for transfers between devices: 9.77 us -> none  [from_everyone(): return lax.all_to_all(copies, axis, split_axis=0, concat_axis=0, tiled=True)]
    unnamed x12, local copies, waits for them, and re-layouts: 3.05 us -> 8.27 us
    all_to_all x1 -> x0, starting transfers between devices: 3.85 us -> none  [from_everyone(): return lax.all_to_all(copies, axis, split_axis=0, concat_axis=0, tiled=True)]
    all_to_all x3 -> x0, other arithmetic: 3.71 us -> none  [the longest x2 2.88 us: from_everyone(): return lax.all_to_all(copies, axis, split_axis=0, concat_axis=0, tiled=True)]
    div x2 -> x0, other arithmetic: 0.87 us -> none  [the longest x1 0.58 us: per_device(): energy = jnp.sum(mode_factors * mode_factors, axis=(2, 3)) / (KX * KY)]
  transfers between devices with their start and end apart: 1 -> 0, of which waited for: 1 -> 0; matrix products, arithmetic and copies ran while one was open for 0% -> 0% of each run, Pallas kernels for 0% -> 0%
where the time goes in v1:
time: 43.4 us; the launch traced here: 43.2 us
  Pallas kernels  34.3 us (79%)
  local copies, waits for them, and re-layouts  8.27 us (19%)
  between operations  0.65 us (1%)
    pallas_call x1, Pallas kernels, per_device(): pl.pallas_call(kernel, out_shape=(jax.ShapeDtypeStruct((LEVELS, VARS, ROW...  34.3 us
    unnamed x12, local copies, waits for them, and re-layouts  8.27 us

profile of v1, /device:TPU:1, one launch (start us, length us, event | category | flops | bytes accessed | tf_op | source)
XLA Modules:
  0.0 43.2 jit_solution(3342627692770471422)
XLA Ops:
  0.6 0.0 copy-start
  0.6 2.3 %copy-done = f32[3,6,128,512]{3,2,1,0:T(8,128)S(1)} copy-done((f32[3,6,128,512]{3,2,1,0:T(8,128)S(1)}, f32[3,6,128,512]{3,2,1,0:T(8,128)}, u32[]{:S(2)}) %copy-start) | copy-done | bytes 4718616
  3.0 0.0 copy-start.1
  3.0 1.7 %copy-done.1 = bf16[3,6,128,512]{3,2,1,0:T(8,128)(2,1)S(1)} copy-done((bf16[3,6,128,512]{3,2,1,0:T(8,128)(2,1)S(1)}, bf16[3,6,128,512]{3,2,1,0:T(8,128)(2,1)}, u32[]{:S(2)}) %copy-start.1) | copy-done | bytes 2359320
  4.6 0.0 copy-start.2
  4.6 0.9 %copy-done.2 = f32[128,512]{1,0:T(8,128)S(1)} copy-done((f32[128,512]{1,0:T(8,128)S(1)}, f32[128,512]{1,0:T(8,128)}, u32[]{:S(2)}) %copy-start.2) | copy-done | bytes 262168
  5.6 0.0 copy-start.3
  5.6 0.7 %copy-done.3 = f32[3,6]{1,0:T(4,128)S(1)} copy-done((f32[3,6]{1,0:T(4,128)S(1)}, f32[3,6]{1,0:T(4,128)}, u32[]{:S(2)}) %copy-start.3) | copy-done | bytes 96
  6.3 0.0 copy-start.4
  6.3 0.7 %copy-done.4 = f32[3]{0:T(128)S(1)} copy-done((f32[3]{0:T(128)S(1)}, f32[3]{0:T(128)}, u32[]{:S(2)}) %copy-start.4) | copy-done | bytes 36
  6.9 34.3 %shard_map.68 = (bf16[3,6,128,512]{3,2,1,0:T(8,128)(2,1)S(1)}, f32[3,6]{1,0:T(4,128)S(1)}) custom-call(f32[3,6,128,512]{3,2,1,0:T(8,128)S(1)} %copy-done, bf16[3,6,128,512]{3,2,1,0:T(8,128)(2,1)S(1)} %copy-done.1, f32[3,6]{1,0:T(4,128)S(1)} %copy-done.3, f32[3]{0:T(128)S(1)} %copy-done.4, f32[128,512]{1,0:T(8,128)S(1)} %copy-done.2), custom_call_target="tpu_custom_call" | custom-call | tf_op jit(solution)/shard_map/pallas_call | solution.py:247
  41.2 1.4 %copy.9 = bf16[3,6,128,512]{3,2,1,0:T(8,128)(2,1)} copy(bf16[3,6,128,512]{3,2,1,0:T(8,128)(2,1)S(1)} %get-tuple-element.4) | data formatting | bytes 4718592
  42.7 0.6 %copy.10 = f32[3,6]{1,0:T(4,128)} copy(f32[3,6]{1,0:T(4,128)S(1)} %get-tuple-element.5) | data formatting | bytes 144
Async XLA Ops:
  0.6 2.3 %copy-start = (f32[3,6,128,512]{3,2,1,0:T(8,128)S(1)}, f32[3,6,128,512]{3,2,1,0:T(8,128)}, u32[]{:S(2)}) copy-start(f32[3,6,128,512]{3,2,1,0:T(8,128)} %prog_hbm.1) | copy-start | bytes 14155780
  3.0 1.7 %copy-start.1 = (bf16[3,6,128,512]{3,2,1,0:T(8,128)(2,1)S(1)}, bf16[3,6,128,512]{3,2,1,0:T(8,128)(2,1)}, u32[]{:S(2)}) copy-start(bf16[3,6,128,512]{3,2,1,0:T(8,128)(2,1)} %forc_hbm.1) | copy-start | bytes 7077892
  4.6 0.9 %copy-start.2 = (f32[128,512]{1,0:T(8,128)S(1)}, f32[128,512]{1,0:T(8,128)}, u32[]{:S(2)}) copy-start(f32[128,512]{1,0:T(8,128)} %pbl_hbm.1) | copy-start | bytes 786436
  5.6 0.7 %copy-start.3 = (f32[3,6]{1,0:T(4,128)S(1)}, f32[3,6]{1,0:T(4,128)}, u32[]{:S(2)}) copy-start(f32[3,6]{1,0:T(4,128)} %strength.1) | copy-start | bytes 220
  6.3 0.7 %copy-start.4 = (f32[3]{0:T(128)S(1)}, f32[3]{0:T(128)}, u32[]{:S(2)}) copy-start(f32[3]{0:T(128)} %height.1) | copy-start | bytes 40
